TPU v7x, 32 devices: a whole 2x2x4 slice. The times are simulated.
32 devices in a mesh: gy: 2 (over core), gx: 16 (over z, y, x).
Axes of the slice: x: 2, y: 2, z: 4, core: 2. Of those that a mesh axis runs over, the one named last changes fastest.
Arguments:
- basis_vectors: float32 [36, 64, 128, 256], P(None, 'gx', 'gy'), may hold values from -30 to 30, as said below
- reaction: float32 [64, 128, 256], P('gx', 'gy'), may hold values from 0.5 to 3
Outputs:
- new_vectors: float32 [4, 64, 128, 256], P(None, 'gx', 'gy')
- hessenberg: float32 [40, 4], replicated
Inputs may be any that keep to these rules, and one draw needn't show every extreme that they name: `basis_vectors`: under the inner product the basis vectors are nearly orthonormal.
All inputs are finite; a program needn't handle non-finite values.
Results may differ from a plain program's by a relative error of at most 0.0003.
Values sent between devices are 32-bit elements; how exact they have to be, the bound alone decides.
A program may use at most 128 MiB of HBM per device.

v0:
```python
import jax
import jax.numpy as jnp
from jax import lax
from jax.sharding import PartitionSpec as P

STEPS = 4


WIND_SPEEDS = (0.9, 0.6, 0.4)
EPSILON = 1e-06


def with_halo(cells, sides, width):
    for axis, dim in sides:
        count = lax.axis_size(axis)
        ends = count - 1
        head = lax.slice_in_dim(cells, 0, width, axis=dim)
        tail = lax.slice_in_dim(cells, cells.shape[dim] - width, cells.shape[dim], axis=dim)
        cells = jnp.concatenate(
            [
                lax.ppermute(tail, axis, [(i, (i + 1) % count) for i in range(ends)]),
                cells,
                lax.ppermute(head, axis, [((i + 1) % count, i) for i in range(ends)]),
            ],
            axis=dim,
        )
    return cells


def stencil(values, x_ext, y_ext, z_ext, reaction):
    summed = -reaction * values
    for position, extended in enumerate((x_ext, y_ext, z_ext)):
        count = values.shape[position]
        higher = lax.slice_in_dim(extended, 3, count + 3, axis=position)
        lower_one = lax.slice_in_dim(extended, 1, count + 1, axis=position)
        lower_two = lax.slice_in_dim(extended, 0, count, axis=position)
        wind_speed = WIND_SPEEDS[position]
        summed = (
            summed
            + higher
            + lower_one
            - 2.0 * values
            - wind_speed * (3.0 * values - 4.0 * lower_one + lower_two) * 0.5
        )
    return summed


def apply_operator(values, reaction):
    rows_x = values.shape[0]
    rows_y = values.shape[1]
    padded = with_halo(values, (("gy", 1), ("gx", 0)), 2)
    x_ext = padded[: rows_x + 3, 2 : rows_y + 2]
    y_ext = padded[2 : rows_x + 2, : rows_y + 3]
    z_ext = jnp.pad(values, ((0, 0), (0, 0), (2, 1)))
    return stencil(values, x_ext, y_ext, z_ext, reaction)


def project(basis_vectors, created, image):
    local = jnp.einsum("kxyz,xyz->k", basis_vectors, image, precision=lax.Precision.HIGHEST)
    extra = [jnp.sum(vector * image)[None] for vector in created]
    return jnp.concatenate([local] + extra)


def combine(basis_vectors, created, weights):
    keep_count = basis_vectors.shape[0]
    summed = jnp.einsum(
        "k,kxyz->xyz", weights[:keep_count], basis_vectors, precision=lax.Precision.HIGHEST
    )
    for index, vector in enumerate(created):
        summed = summed + weights[keep_count + index] * vector
    return summed


def body(basis_vectors, reaction):
    keep_count = basis_vectors.shape[0]
    basis_size = keep_count + STEPS
    cell_count = float(
        basis_vectors.shape[1]
        * basis_vectors.shape[2]
        * basis_vectors.shape[3]
        * lax.axis_size("gx")
        * lax.axis_size("gy")
    )
    created = []
    columns = []
    local_gram = jnp.einsum(
        "axyz,bxyz->ab", basis_vectors, basis_vectors, precision=lax.Precision.HIGHEST
    )
    kept_gram = lax.psum(local_gram, ("gy", "gx")) / cell_count
    gram_matrix = (
        jnp.zeros((basis_size, basis_size), jnp.float32).at[:keep_count, :keep_count].set(kept_gram)
    )
    for section in range(STEPS):
        current = keep_count + section
        vector_now = basis_vectors[keep_count - 1] if section == 0 else created[-1]
        image = apply_operator(vector_now, reaction)
        first_terms = lax.psum(project(basis_vectors, created, image), ("gy", "gx")) / cell_count
        first_rest = image - combine(basis_vectors, created, first_terms)
        second_terms, rest_square = lax.psum(
            (project(basis_vectors, created, first_rest), jnp.sum(first_rest * first_rest)),
            ("gy", "gx"),
        )
        second_terms = second_terms / cell_count
        rest_square = rest_square / cell_count
        gram_now = gram_matrix[:current, :current]
        folded = jnp.dot(gram_now, second_terms, precision=lax.Precision.HIGHEST)
        second_rest = first_rest - combine(basis_vectors, created, second_terms)
        squared = (
            rest_square
            - 2.0 * jnp.sum(second_terms * second_terms)
            + jnp.sum(second_terms * folded)
        )
        length_now = jnp.sqrt(squared + EPSILON)
        cross_terms = (second_terms - folded) / length_now
        gram_matrix = gram_matrix.at[:current, current].set(cross_terms)
        gram_matrix = gram_matrix.at[current, :current].set(cross_terms)
        gram_matrix = gram_matrix.at[current, current].set(squared / (length_now * length_now))
        weights = first_terms + second_terms
        columns.append(
            jnp.concatenate(
                [weights, length_now[None], jnp.zeros((basis_size - current - 1,), jnp.float32)]
            )
        )
        created.append(second_rest / length_now)
    return (jnp.stack(created), jnp.stack(columns, axis=1))


def solution(mesh):
    in_specs = (P(None, "gx", "gy", None), P("gx", "gy", None))
    out_specs = (P(None, "gx", "gy", None), P())
    return jax.shard_map(body, mesh=mesh, in_specs=in_specs, out_specs=out_specs, check_vma=False)
```

profile of v0, /device:TPU:0, one launch (start us, length us, event | category | flops | bytes accessed | tf_op | source)
XLA Modules:
  0.0 709.3 jit_solution(1123148927254146616)
XLA Ops:
  6.6 25.4 %fusion.34 = f32[36,36]{1,0:T(8,128)S(1)} fusion(f32[36,4,64,256]{3,2,1,0:T(8,128)} %param.22), kind=kOutput, calls=%fused_computation.34 | convolution fusion | flops 1019215872 | bytes 9442368 | tf_op jit(solution)/shard_map/axyz,bxyz->ab/dot_general | solution.py:86
  61.3 42.1 %psum.91 = f32[36]{0:T(128)S(1)} all-reduce(f32[36]{0:T(128)S(1)} %fusion.38), channel_id=1, replica_groups=mesh['gy'=2,'gx'=16] {'gy','gx'}, use_global_device_ids=true, to_apply=%region_0.0 | all-reduce | flops 36 | bytes 288 | tf_op jit(solution)/shard_map/psum | solution.py:97
  103.4 14.5 %fusion.26 = f32[1,4,64,256]{3,0,2,1:T(1,128)S(1)} fusion(f32[36,4,64,256]{3,2,1,0:T(8,128)} %param.22, f32[36]{0:T(128)S(1)} %psum.91), kind=kOutput, calls=%fused_computation.26 | convolution fusion | flops 28311588 | bytes 9699472 | tf_op jit(solution)/shard_map/k,kxyz->xyz/dot_general | solution.py:66
  118.6 15.8 %fusion.41 = f32[36]{0:T(128)S(1)} fusion(f32[36,4,64,256]{3,2,1,0:T(8,128)} %param.22, f32[4,64,256,1]{2,1,0,3:T(8,128)S(1)} %get-tuple-element.159), kind=kOutput, calls=%fused_computation.41 | convolution fusion | flops 28311552 | bytes 9699472 | tf_op jit(solution)/shard_map/kxyz,xyz->k/dot_general | solution.py:59
  134.4 39.9 %all-reduce.8 = (f32[36]{0:T(128)S(1)}, f32[]{:T(128)}, f32[36,36]{1,0:T(8,128)S(1)}) all-reduce(f32[36]{0:T(128)S(1)} %fusion.41, f32[]{:T(128)} %get-tuple-element.158, f32[36,36]{1,0:T(8,128)S(1)} %fusion.34), channel_id=1, replica_groups=mesh['gy'=2,'gx'=16] {'gy','gx'}, use_global_device_ids=true, to_apply=%region_1.0 | all-reduce | flops 1333 | bytes 10664 | tf_op jit(solution)/shard_map/psum | solution.py:99
  175.1 14.5 %fusion.22 = f32[1,4,64,256]{3,0,2,1:T(1,128)S(1)} fusion(f32[36,4,64,256]{3,2,1,0:T(8,128)} %param.22, f32[36]{0:T(128)S(1)} %get-tuple-element.148), kind=kOutput, calls=%fused_computation.22 | convolution fusion | flops 28311588 | bytes 9699472 | tf_op jit(solution)/shard_map/k,kxyz->xyz/dot_general | solution.py:66
  210.2 16.0 %fusion.44 = f32[36]{0:T(128)S(1)} fusion(f32[36,4,64,256]{3,2,1,0:T(8,128)} %param.22, f32[4,64,256,1]{2,1,0,3:T(8,128)S(1)} %bitcast.241), kind=kOutput, calls=%fused_computation.42 | convolution fusion | flops 28311552 | bytes 9699472 | tf_op jit(solution)/shard_map/kxyz,xyz->k/dot_general | solution.py:59
  226.9 41.7 %psum.95 = f32[37]{0:T(128)S(1)} all-reduce(f32[37]{0:T(128)S(1)} %pad_maximum_fusion.26), channel_id=1, replica_groups=mesh['gy'=2,'gx'=16] {'gy','gx'}, use_global_device_ids=true, to_apply=%region_8.9 | all-reduce | flops 37 | bytes 296 | tf_op jit(solution)/shard_map/psum | solution.py:97
  269.2 14.5 %fusion.18 = f32[1,4,64,256]{3,0,2,1:T(1,128)S(1)} fusion(f32[36,4,64,256]{3,2,1,0:T(8,128)} %param.22, f32[37]{0:T(128)S(1)} %broadcast_multiply_fusion.6), kind=kOutput, calls=%fused_computation.18 | convolution fusion | flops 28311552 | bytes 9699476 | tf_op jit(solution)/shard_map/k,kxyz->xyz/dot_general | solution.py:66
  285.1 16.1 %fusion.47 = f32[36]{0:T(128)S(1)} fusion(f32[36,4,64,256]{3,2,1,0:T(8,128)} %param.22, f32[4,64,256,1]{2,1,0,3:T(8,128)S(1)} %bitcast.236), kind=kOutput, calls=%fused_computation.43 | convolution fusion | flops 28311552 | bytes 9699472 | tf_op jit(solution)/shard_map/kxyz,xyz->k/dot_general | solution.py:59
  301.9 39.9 %all-reduce.7 = (f32[37]{0:T(128)S(1)}, f32[]{:T(128)}) all-reduce(f32[37]{0:T(128)S(1)} %pad_maximum_fusion.27, f32[]{:T(128)} %get-tuple-element.134), channel_id=1, replica_groups=mesh['gy'=2,'gx'=16] {'gy','gx'}, use_global_device_ids=true, to_apply=%region_10.11 | all-reduce | flops 38 | bytes 304 | tf_op jit(solution)/shard_map/psum | solution.py:99
  345.1 14.5 %fusion.14 = f32[1,4,64,256]{3,0,2,1:T(1,128)S(1)} fusion(f32[36,4,64,256]{3,2,1,0:T(8,128)} %param.22, f32[37]{0:T(128)S(1)} %get-tuple-element.197), kind=kOutput, calls=%fused_computation.14 | convolution fusion | flops 28311552 | bytes 9699476 | tf_op jit(solution)/shard_map/k,kxyz->xyz/dot_general | solution.py:66
  379.4 16.3 %fusion.50 = f32[36]{0:T(128)S(1)} fusion(f32[36,4,64,256]{3,2,1,0:T(8,128)} %param.22, f32[4,64,256,1]{2,1,0,3:T(8,128)S(1)} %bitcast.240), kind=kOutput, calls=%fused_computation.44 | convolution fusion | flops 28311552 | bytes 9699472 | tf_op jit(solution)/shard_map/kxyz,xyz->k/dot_general | solution.py:59
  397.1 41.7 %psum.98 = f32[38]{0:T(128)S(1)} all-reduce(f32[38]{0:T(128)S(1)} %pad_maximum_fusion.28), channel_id=1, replica_groups=mesh['gy'=2,'gx'=16] {'gy','gx'}, use_global_device_ids=true, to_apply=%region_18.19 | all-reduce | flops 38 | bytes 304 | tf_op jit(solution)/shard_map/psum | solution.py:97
  439.5 14.5 %fusion.10 = f32[1,4,64,256]{3,0,2,1:T(1,128)S(1)} fusion(f32[36,4,64,256]{3,2,1,0:T(8,128)} %param.22, f32[38]{0:T(128)S(1)} %broadcast_multiply_fusion.4), kind=kOutput, calls=%fused_computation.10 | convolution fusion | flops 28311552 | bytes 9699480 | tf_op jit(solution)/shard_map/k,kxyz->xyz/dot_general | solution.py:66
  456.0 16.0 %fusion.53 = f32[36]{0:T(128)S(1)} fusion(f32[36,4,64,256]{3,2,1,0:T(8,128)} %param.22, f32[4,64,256,1]{2,1,0,3:T(8,128)S(1)} %bitcast.239), kind=kOutput, calls=%fused_computation.45 | convolution fusion | flops 28311552 | bytes 9699472 | tf_op jit(solution)/shard_map/kxyz,xyz->k/dot_general | solution.py:59
  473.3 39.1 %all-reduce.6 = (f32[38]{0:T(128)S(1)}, f32[]{:T(128)}) all-reduce(f32[38]{0:T(128)S(1)} %pad_maximum_fusion.29, f32[]{:T(128)} %get-tuple-element.129), channel_id=1, replica_groups=mesh['gy'=2,'gx'=16] {'gy','gx'}, use_global_device_ids=true, to_apply=%region_21.22 | all-reduce | flops 39 | bytes 312 | tf_op jit(solution)/shard_map/psum | solution.py:99
  515.9 14.5 %fusion.6 = f32[1,4,64,256]{3,0,2,1:T(1,128)S(1)} fusion(f32[36,4,64,256]{3,2,1,0:T(8,128)} %param.22, f32[38]{0:T(128)S(1)} %get-tuple-element.188), kind=kOutput, calls=%fused_computation.6 | convolution fusion | flops 28311552 | bytes 9699480 | tf_op jit(solution)/shard_map/k,kxyz->xyz/dot_general | solution.py:66
  551.9 16.3 %fusion.56 = f32[36]{0:T(128)S(1)} fusion(f32[36,4,64,256]{3,2,1,0:T(8,128)} %param.22, f32[4,64,256,1]{2,1,0,3:T(8,128)S(1)} %bitcast.237), kind=kOutput, calls=%fused_computation.46 | convolution fusion | flops 28311552 | bytes 9699472 | tf_op jit(solution)/shard_map/kxyz,xyz->k/dot_general | solution.py:59
  570.2 41.5 %psum.101 = f32[39]{0:T(128)S(1)} all-reduce(f32[39]{0:T(128)S(1)} %pad_maximum_fusion.30), channel_id=1, replica_groups=mesh['gy'=2,'gx'=16] {'gy','gx'}, use_global_device_ids=true, to_apply=%region_30.31 | all-reduce | flops 39 | bytes 312 | tf_op jit(solution)/shard_map/psum | solution.py:97
  612.3 14.5 %fusion.2 = f32[1,4,64,256]{3,0,2,1:T(1,128)S(1)} fusion(f32[36,4,64,256]{3,2,1,0:T(8,128)} %param.22, f32[39]{0:T(128)S(1)} %broadcast_multiply_fusion.2), kind=kOutput, calls=%fused_computation.2 | convolution fusion | flops 28311552 | bytes 9699484 | tf_op jit(solution)/shard_map/k,kxyz->xyz/dot_general | solution.py:66
  629.6 16.0 %fusion.59 = f32[36]{0:T(128)S(1)} fusion(f32[36,4,64,256]{3,2,1,0:T(8,128)} %param.22, f32[4,64,256,1]{2,1,0,3:T(8,128)S(1)} %bitcast.238), kind=kOutput, calls=%fused_computation.47 | convolution fusion | flops 28311552 | bytes 9699472 | tf_op jit(solution)/shard_map/kxyz,xyz->k/dot_general | solution.py:59
  647.6 39.2 %all-reduce.5 = (f32[39]{0:T(128)S(1)}, f32[]{:T(128)}) all-reduce(f32[39]{0:T(128)S(1)} %pad_maximum_fusion.31, f32[]{:T(128)} %get-tuple-element.122), channel_id=1, replica_groups=mesh['gy'=2,'gx'=16] {'gy','gx'}, use_global_device_ids=true, to_apply=%region_34.35 | all-reduce | flops 40 | bytes 320 | tf_op jit(solution)/shard_map/psum | solution.py:99
  688.1 14.5 %fusion.28 = f32[1,4,64,256]{3,0,2,1:T(1,128)S(1)} fusion(f32[36,4,64,256]{3,2,1,0:T(8,128)} %param.22, f32[39]{0:T(128)S(1)} %get-tuple-element.181), kind=kOutput, calls=%fused_computation.28 | convolution fusion | flops 28311552 | bytes 9699484 | tf_op jit(solution)/shard_map/k,kxyz->xyz/dot_general | solution.py:66
  (129 shorter events, 121.1 us)
Async XLA Ops:
  0.6 31.3 %copy-start.2 = (s32[2]{0:T(128)S(1)}, s32[2]{0:T(128)}, u32[]{:S(2)}) copy-start(s32[2]{0:T(128)} %constant.309.clone.1) | copy-start | bytes 28
  0.6 32.0 %copy-start.4 = (s32[2]{0:T(128)S(1)}, s32[2]{0:T(128)}, u32[]{:S(2)}) copy-start(s32[2]{0:T(128)} %constant.307.clone.1) | copy-start | bytes 28
  0.7 32.7 %copy-start.3 = (s32[2]{0:T(128)S(1)}, s32[2]{0:T(128)}, u32[]{:S(2)}) copy-start(s32[2]{0:T(128)} %constant.304.clone.1) | copy-start | bytes 28
  0.7 46.9 %copy-start = (f32[36,4,64,256]{3,2,1,0:T(8,128)S(1)}, f32[36,4,64,256]{3,2,1,0:T(8,128)}, u32[]{:S(2)}) copy-start(f32[36,4,64,256]{3,2,1,0:T(8,128)} %param.22) | copy-start | bytes 28311556
  0.7 46.5 %copy-start.1 = (f32[4,64,256]{2,1,0:T(8,128)S(1)}, f32[4,64,256]{2,1,0:T(8,128)}, u32[]{:S(2)}) copy-start(f32[4,64,256]{2,1,0:T(8,128)} %param.23) | copy-start | bytes 786436
  1.8 32.7 %collective-permute-start.1 = (f32[4,2,256]{2,1,0:T(2,128)S(1)}, f32[4,2,256]{2,1,0:T(2,128)S(1)}, u32[]{:S(2)}, u32[]{:S(2)}) collective-permute-start(f32[4,2,256]{2,1,0:T(2,128)S(1)} %get-tuple-element.174), channel_id=1, source_target_pairs={{16,0},{17,1},{18,2},{19,3},{20,4},{21,5},{22,6},{23,7},{24,8},{25... | collective-permute-start | bytes 24584 | tf_op jit(solution)/shard_map/ppermute | solution.py:23
  3.4 31.2 %collective-permute-start = (f32[4,2,256]{2,1,0:T(2,128)S(1)}, f32[4,2,256]{2,1,0:T(2,128)S(1)}, u32[]{:S(2)}, u32[]{:S(2)}) collective-permute-start(f32[4,2,256]{2,1,0:T(2,128)S(1)} %get-tuple-element.175), channel_id=1, source_target_pairs={{0,16},{1,17},{2,18},{3,19},{4,20},{5,21},{6,22},{7,23},{8,24},{9,... | collective-permute-start | bytes 24584 | tf_op jit(solution)/shard_map/ppermute | solution.py:21
  34.7 7.4 %collective-permute-start.3 = (f32[2,68,256]{2,1,0:T(8,128)S(1)}, f32[2,68,256]{2,1,0:T(8,128)S(1)}, u32[]{:S(2)}, u32[]{:S(2)}) collective-permute-start(f32[2,68,256]{2,1,0:T(8,128)S(1)} %get-tuple-element.167), channel_id=1, source_target_pairs={{0,1},{1,2},{2,3},{3,4},{4,5},{5,6},{6,7},{7,8},{8,9},{9,10},{10,1... | collective-permute-start | bytes 417800 | tf_op jit(solution)/shard_map/ppermute | solution.py:21
  40.0 7.1 %collective-permute-start.2 = (f32[2,68,256]{2,1,0:T(8,128)S(1)}, f32[2,68,256]{2,1,0:T(8,128)S(1)}, u32[]{:S(2)}, u32[]{:S(2)}) collective-permute-start(f32[2,68,256]{2,1,0:T(8,128)S(1)} %get-tuple-element.166), channel_id=1, source_target_pairs={{1,0},{2,1},{3,2},{4,3},{5,4},{6,5},{7,6},{8,7},{9,8},{10,9},{11,1... | collective-permute-start | bytes 417800 | tf_op jit(solution)/shard_map/ppermute | solution.py:23
  191.7 4.5 collective-permute-start.5
  193.0 3.8 collective-permute-start.4
  196.9 12.3 %collective-permute-start.6 = (f32[2,68,256]{2,1,0:T(8,128)S(1)}, f32[2,68,256]{2,1,0:T(8,128)S(1)}, u32[]{:S(2)}, u32[]{:S(2)}) collective-permute-start(f32[2,68,256]{2,1,0:T(8,128)S(1)} %get-tuple-element.164), channel_id=1, source_target_pairs={{1,0},{2,1},{3,2},{4,3},{5,4},{6,5},{7,6},{8,7},{9,8},{10,9},{11,1... | collective-permute-start | bytes 417800 | tf_op jit(solution)/shard_map/ppermute | solution.py:23
  198.2 10.9 %collective-permute-start.7 = (f32[2,68,256]{2,1,0:T(8,128)S(1)}, f32[2,68,256]{2,1,0:T(8,128)S(1)}, u32[]{:S(2)}, u32[]{:S(2)}) collective-permute-start(f32[2,68,256]{2,1,0:T(8,128)S(1)} %get-tuple-element.165), channel_id=1, source_target_pairs={{0,1},{1,2},{2,3},{3,4},{4,5},{5,6},{6,7},{7,8},{8,9},{9,10},{10,1... | collective-permute-start | bytes 417800 | tf_op jit(solution)/shard_map/ppermute | solution.py:21
  360.2 4.5 collective-permute-start.9
  361.5 3.8 collective-permute-start.8
  365.4 12.9 %collective-permute-start.10 = (f32[2,68,256]{2,1,0:T(8,128)S(1)}, f32[2,68,256]{2,1,0:T(8,128)S(1)}, u32[]{:S(2)}, u32[]{:S(2)}) collective-permute-start(f32[2,68,256]{2,1,0:T(8,128)S(1)} %get-tuple-element.162), channel_id=1, source_target_pairs={{1,0},{2,1},{3,2},{4,3},{5,4},{6,5},{7,6},{8,7},{9,8},{10,9},{11,1... | collective-permute-start | bytes 417800 | tf_op jit(solution)/shard_map/ppermute | solution.py:23
  366.7 11.6 %collective-permute-start.11 = (f32[2,68,256]{2,1,0:T(8,128)S(1)}, f32[2,68,256]{2,1,0:T(8,128)S(1)}, u32[]{:S(2)}, u32[]{:S(2)}) collective-permute-start(f32[2,68,256]{2,1,0:T(8,128)S(1)} %get-tuple-element.163), channel_id=1, source_target_pairs={{0,1},{1,2},{2,3},{3,4},{4,5},{5,6},{6,7},{7,8},{8,9},{9,10},{10,1... | collective-permute-start | bytes 417800 | tf_op jit(solution)/shard_map/ppermute | solution.py:21
  531.7 4.5 collective-permute-start.13
  533.0 3.8 collective-permute-start.12
  536.9 9.6 %collective-permute-start.15 = (f32[2,68,256]{2,1,0:T(8,128)S(1)}, f32[2,68,256]{2,1,0:T(8,128)S(1)}, u32[]{:S(2)}, u32[]{:S(2)}) collective-permute-start(f32[2,68,256]{2,1,0:T(8,128)S(1)} %get-tuple-element.161), channel_id=1, source_target_pairs={{0,1},{1,2},{2,3},{3,4},{4,5},{5,6},{6,7},{7,8},{8,9},{9,10},{10,1... | collective-permute-start | bytes 417800 | tf_op jit(solution)/shard_map/ppermute | solution.py:21
  543.0 7.7 %collective-permute-start.14 = (f32[2,68,256]{2,1,0:T(8,128)S(1)}, f32[2,68,256]{2,1,0:T(8,128)S(1)}, u32[]{:S(2)}, u32[]{:S(2)}) collective-permute-start(f32[2,68,256]{2,1,0:T(8,128)S(1)} %get-tuple-element.160), channel_id=1, source_target_pairs={{1,0},{2,1},{3,2},{4,3},{5,4},{6,5},{7,6},{8,7},{9,8},{10,9},{11,1... | collective-permute-start | bytes 417800 | tf_op jit(solution)/shard_map/ppermute | solution.py:23
where the time goes:
time: 720 us; the launch traced here: 709 us
  blocking collectives  325 us (45%)
  matrix products  270 us (38%)
  starting transfers between devices  41.6 us (6%)
  other arithmetic  33.5 us (5%)
  waiting for transfers between devices  16.6 us (2%)
  local copies, waits for them, and re-layouts  13.3 us (2%)
  between operations  9.55 us (1%)
    psum x4, blocking collectives, body(): lax.psum(project(basis_vectors, created, image), ('gy', 'gx')) / cell_count  167 us
    psum x4, blocking collectives, body(): lax.psum((project(basis_vectors, created, first_rest), jnp.sum(first_rest...  158 us
    dot_general x8, matrix products, project(): jnp.einsum('kxyz,xyz->k', basis_vectors, image, precision=lax.Precision.H...  126 us
    dot_general x8, matrix products, combine(): jnp.einsum('k,kxyz->xyz', weights[:keep_count], basis_vectors, precision=...  116 us
    ppermute x8, starting transfers between devices, with_halo(): lax.ppermute(tail, axis, [(i, (i + 1) % count) for i in range(ends)])  30.8 us
    dot_general x1, matrix products, body(): jnp.einsum('axyz,bxyz->ab', basis_vectors, basis_vectors, precision=lax.P...  25.4 us
  transfers between devices with their start and end apart: 16, of which 8 were waited for; matrix products, arithmetic and copies ran while one was open for 6% of the time, Pallas kernels for 0%

commit v1 on v0

v1 whole, which is shorter than its diff:
```python
import functools

import jax
import jax.numpy as jnp
from jax import lax
from jax.experimental import pallas as pl
from jax.experimental.pallas import tpu as pltpu
from jax.sharding import PartitionSpec as P

STEPS = 4
WIND_SPEEDS = (0.9, 0.6, 0.4)
EPSILON = 1e-06
MESH = pl.DeviceIdType.MESH
BLOCK = 6
LOADS = 6


def roll(values, shift, axis):
    return pltpu.roll(values, shift, axis)


def fold_lanes(values):
    parts = [values[:, s : s + 128] for s in range(0, values.shape[1], 128)]
    return functools.reduce(lambda a, b: a + b, parts)


def kernel(
    keep, planes, rows_y, n_gx, n_gy, g1,
    basis, reaction, w_out, h_out,
    vecs, padded, image, react, gram_rows, proj_rows, slots1, slots2, coef,
    load_sem, last_sem, react_sem, out_sem,
    halo_send, halo_recv, send1, recv1, send2, recv2,
):
    width = basis.shape[2]
    rows = planes * rows_y
    padded_count = proj_rows.shape[1]
    gx = lax.axis_index("gx")
    gy = lax.axis_index("gy")
    n1 = n_gy * g1
    n2 = n_gx // g1
    low = lax.rem(gx, g1)
    high = gx // g1
    me1 = gy * g1 + low
    me2 = high
    cells = float(rows * width * n_gx * n_gy)

    last_copies = [
        pltpu.make_async_copy(
            basis.at[keep - 1, p * rows_y : (p + 1) * rows_y],
            padded.at[0, p + 2, 8 : rows_y + 8],
            last_sem.at[p],
        )
        for p in range(planes)
    ]
    for copy in last_copies:
        copy.start()
    bounds = [(g * keep // LOADS, (g + 1) * keep // LOADS) for g in range(LOADS)]
    loads = [
        pltpu.make_async_copy(basis.at[a:b], vecs.at[a:b], load_sem.at[g])
        for g, (a, b) in enumerate(bounds)
    ]
    for copy in loads:
        copy.start()
    react_copy = pltpu.make_async_copy(reaction, react, react_sem)
    react_copy.start()

    has_xl, has_xh = gx > 0, gx < n_gx - 1
    has_yl, has_yh = gy > 0, gy < n_gy - 1

    def member1(d):
        p = lax.rem(me1 + d, n1)
        return p, {"gx": high * g1 + lax.rem(p, g1), "gy": p // g1}

    def member2(d):
        p = lax.rem(me2 + d, n2)
        return p, {"gx": p * g1 + low, "gy": gy}

    barrier = pltpu.get_barrier_semaphore()
    for d in range(1, n1):
        pl.semaphore_signal(barrier, inc=1, device_id=member1(d)[1], device_id_type=MESH)
    for d in range(1, n2):
        pl.semaphore_signal(barrier, inc=1, device_id=member2(d)[1], device_id_type=MESH)
    sides = (
        (has_xh, {"gx": gx + 1, "gy": gy}),
        (has_xl, {"gx": gx - 1, "gy": gy}),
        (has_yh, {"gx": gx, "gy": gy + 1}),
        (has_yl, {"gx": gx, "gy": gy - 1}),
    )
    expected = n1 - 1 + n2 - 1
    for there, device in sides:
        @pl.when(there)
        def _(device=device):
            pl.semaphore_signal(barrier, inc=1, device_id=device, device_id_type=MESH)

        expected = expected + there.astype(jnp.int32)

    zero_plane = jnp.zeros((1, rows_y, width), jnp.float32)
    zero_rows = jnp.zeros((planes, 8, width), jnp.float32)
    for step in range(STEPS):
        @pl.when(jnp.logical_not(has_xl))
        def _(step=step):
            padded[step, 0:1, 8 : rows_y + 8] = zero_plane
            padded[step, 1:2, 8 : rows_y + 8] = zero_plane

        @pl.when(jnp.logical_not(has_xh))
        def _(step=step):
            padded[step, planes + 2 : planes + 3, 8 : rows_y + 8] = zero_plane

        @pl.when(jnp.logical_not(has_yl))
        def _(step=step):
            padded[step, 2 : planes + 2, 0:8] = zero_rows

        @pl.when(jnp.logical_not(has_yh))
        def _(step=step):
            padded[step, 2 : planes + 2, rows_y + 8 : rows_y + 16] = zero_rows

    gram_rows[...] = jnp.zeros(gram_rows.shape, jnp.float32)
    proj_rows[...] = jnp.zeros(proj_rows.shape, jnp.float32)
    pl.semaphore_wait(barrier, expected)

    def halo_copies(step):
        own = pl.ds(2, planes)
        refs = (
            (padded.at[step, planes : planes + 2, 8 : rows_y + 8], padded.at[step, 0:2, 8 : rows_y + 8]),
            (padded.at[step, 2:3, 8 : rows_y + 8], padded.at[step, planes + 2 : planes + 3, 8 : rows_y + 8]),
            (padded.at[step, own, rows_y : rows_y + 8], padded.at[step, own, 0:8]),
            (padded.at[step, own, 8:16], padded.at[step, own, rows_y + 8 : rows_y + 16]),
        )
        return [
            pltpu.make_async_remote_copy(
                src_ref=src, dst_ref=dst,
                send_sem=halo_send.at[step, n], recv_sem=halo_recv.at[step, n],
                device_id=sides[n][1], device_id_type=MESH,
            )
            for n, (src, dst) in enumerate(refs)
        ]

    def start_halo(step):
        for n, copy in enumerate(halo_copies(step)):
            @pl.when(sides[n][0])
            def _(copy=copy):
                copy.start()

    def wait_halo(step):
        copies = halo_copies(step)
        arrives = (has_xl, has_xh, has_yl, has_yh)
        for n, copy in enumerate(copies):
            @pl.when(arrives[n])
            def _(copy=copy):
                copy.wait_recv()

            @pl.when(sides[n][0])
            def _(copy=copy):
                copy.wait_send()

    def exchange(rnd, slots, me, count, member, send, recv, start, stop):
        def copy_of(slot, d):
            return pltpu.make_async_remote_copy(
                src_ref=slots.at[rnd, slot, start:stop], dst_ref=slots.at[rnd, slot, start:stop],
                send_sem=send.at[rnd, d - 1], recv_sem=recv.at[rnd, slot],
                device_id=member(d)[1], device_id_type=MESH,
            )

        for d in range(1, count):
            copy_of(me, d).start()
        for d in range(1, count):
            copy_of(member(d)[0], d).wait_recv()
        for d in range(1, count):
            copy_of(me, d).wait_send()
        total = slots[rnd, 0, start:stop]
        for slot in range(1, count):
            total = total + slots[rnd, slot, start:stop]
        return total

    def all_sum(rnd, start, stop):
        total = exchange(rnd, slots1, me1, n1, member1, send1, recv1, start, stop)
        if n2 > 1:
            slots2[rnd, me2, start:stop] = total
            total = exchange(rnd, slots2, me2, n2, member2, send2, recv2, start, stop)
        return total / cells

    shape = (padded_count, 128)
    lane = lax.broadcasted_iota(jnp.int32, shape, 1)
    sub = lax.broadcasted_iota(jnp.int32, shape, 0)
    eye = lane == sub
    sub8 = lax.broadcasted_iota(jnp.int32, (8, 128), 0)

    def lane_sum(values):
        return jnp.broadcast_to(jnp.sum(values, axis=1, keepdims=True), values.shape)

    def to_column(row):
        return lane_sum(jnp.where(eye, jnp.broadcast_to(row, shape), 0.0))

    def to_row(column):
        return jnp.sum(jnp.where(eye, column, 0.0), axis=0, keepdims=True)

    def project(load, count, kind):
        for first in range(0, count, 20):
            group = range(first, min(first + 20, count))

            def step(r, sums):
                at = pl.ds(pl.multiple_of(r * 8, 8), 8)
                other = load(at)
                return tuple(
                    acc + fold_lanes(vecs[i, at, :] * other) for i, acc in zip(group, sums)
                )

            zero = jnp.zeros((8, 128), jnp.float32)
            sums = lax.fori_loop(0, rows // 8, step, (zero,) * len(group))
            for i, acc in zip(group, sums):
                proj_rows[kind, i : i + 1, :] = jnp.sum(acc, axis=0, keepdims=True)

    def stencil(step):
        tall = 16
        lanes = lax.broadcasted_iota(jnp.int32, (tall, width), 1)
        sx, sy, sz = WIND_SPEEDS
        centre = 6.0 + 1.5 * (sx + sy + sz)

        def piece(p, q):
            base = pl.multiple_of(q * tall, 8)
            at = pl.ds(pl.multiple_of(base + 8, 8), tall)
            block = padded[step, p + 2, pl.ds(base, tall + 16), :]
            here = block[8 : tall + 8]
            out_at = pl.ds(pl.multiple_of(p * rows_y + base, 8), tall)
            total = -(react[out_at, :] + centre) * here
            total = total + padded[step, p + 3, at, :]
            total = total + (1.0 + 2.0 * sx) * padded[step, p + 1, at, :]
            total = total - (0.5 * sx) * padded[step, p, at, :]
            total = total + roll(block, tall + 15, 0)[8 : tall + 8]
            total = total + (1.0 + 2.0 * sy) * roll(block, 1, 0)[8 : tall + 8]
            total = total - (0.5 * sy) * roll(block, 2, 0)[8 : tall + 8]
            total = total + jnp.where(lanes < width - 1, roll(here, width - 1, 1), 0.0)
            total = total + (1.0 + 2.0 * sz) * jnp.where(lanes >= 1, roll(here, 1, 1), 0.0)
            total = total - (0.5 * sz) * jnp.where(lanes >= 2, roll(here, 2, 1), 0.0)
            image[out_at, :] = total

        @pl.loop(0, planes)
        def _(p):
            @pl.loop(0, rows_y // tall)
            def _(q):
                piece(p, q)

    def combine(step, count, scale):
        tall = 16
        scale_row = jnp.concatenate([scale] * (width // 128), axis=1)

        @pl.loop(0, planes)
        def _(p):
            @pl.loop(0, rows_y // tall)
            def _(q):
                at = pl.ds(pl.multiple_of(p * rows_y + q * tall, 8), tall)
                total = image[at, :] * scale_row
                for i in range(count):
                    total = total - coef[i : i + 1, :] * vecs[i, at, :]
                vecs[keep + step, at, :] = total
                if step < STEPS - 1:
                    padded[step + 1, p + 2, pl.ds(pl.multiple_of(q * tall + 8, 8), tall), :] = total

    def send_row(rnd, a_row, b_row):
        slots1[rnd, me1, padded_count : padded_count + 8] = jnp.where(
            sub8 == 0, a_row, jnp.where(sub8 == 1, b_row, 0.0)
        )

    for copy in last_copies:
        copy.wait()
    start_halo(0)
    ready = 0
    blocks = [(s, min(s + BLOCK, keep)) for s in range(0, keep, BLOCK)]
    for jb in range(len(blocks)):
        while ready < LOADS and bounds[ready][0] < blocks[jb][1]:
            loads[ready].wait()
            ready += 1
        for ib in range(jb + 1):
            pairs = [
                (i, j)
                for i in range(*blocks[ib])
                for j in range(*blocks[jb])
                if i <= j
            ]

            def step(r, sums, ib=ib, jb=jb, pairs=pairs):
                at = pl.ds(pl.multiple_of(r * 8, 8), 8)
                for s in range(0, width, 128):
                    needed = sorted(set(range(*blocks[ib])) | set(range(*blocks[jb])))
                    held = {i: vecs[i, at, s : s + 128] for i in needed}
                    sums = tuple(acc + held[i] * held[j] for (i, j), acc in zip(pairs, sums))
                return sums

            zero = jnp.zeros((8, 128), jnp.float32)
            sums = lax.fori_loop(0, rows // 8, step, (zero,) * len(pairs))
            for (i, j), acc in zip(pairs, sums):
                line = jnp.sum(acc, axis=0, keepdims=True)
                gram_rows[i, j : j + 1, :] = line
                if i != j:
                    gram_rows[j, i : i + 1, :] = line
    local_gram = jnp.zeros(shape, jnp.float32)
    for i in range(keep):
        local_gram = jnp.where(lane == i, lane_sum(gram_rows[i]), local_gram)
    slots1[0, me1, 0:padded_count] = local_gram
    react_copy.wait()

    gram = None
    scales = jnp.ones(shape, jnp.float32)
    hess = jnp.zeros(shape, jnp.float32)
    b_row = jnp.zeros((1, 128), jnp.float32)
    out_copies = []
    for step in range(STEPS):
        count = keep + step
        last = count - 1
        if step > 0:
            project(lambda at: vecs[last, at, :], count, 1)
            b_row = to_row(lane_sum(proj_rows[1]))
        wait_halo(step)
        stencil(step)
        project(lambda at: image[at, :], count, 0)
        send_row(step, to_row(lane_sum(proj_rows[0])), b_row)
        if step == 0:
            total = all_sum(0, 0, padded_count + 8)
            gram = total[0:padded_count]
            total = total[padded_count:]
            scale = jnp.ones((1, 128), jnp.float32)
        else:
            total = all_sum(step, padded_count, padded_count + 8)
            overlap = to_column(total[1:2])
            norm = jnp.sqrt(overlap[last : last + 1] + EPSILON)
            scale = 1.0 / norm
            hess = jnp.where((lane == step - 1) & (sub == last), norm, hess)
            scales = jnp.where(sub == last, scale, scales)
            column = jnp.where(sub < count, overlap * scales * scale, 0.0)
            gram = jnp.where(sub == last, to_row(column), gram)
            gram = jnp.where(lane == last, column, gram)
        first = jnp.where(sub < count, to_column(total[0:1]) * scales * scale, 0.0)
        weights = first + (first - lane_sum(gram * to_row(first)))
        weights = jnp.where(sub < count, weights, 0.0)
        hess = jnp.where((lane == step) & (sub < count), weights, hess)
        scaled = weights * scales
        coef[...] = jnp.concatenate([scaled] * (width // 128), axis=1)
        combine(step, count, scale)
        if step < STEPS - 1:
            start_halo(step + 1)
        copy = pltpu.make_async_copy(vecs.at[keep + step], w_out.at[step], out_sem.at[step])
        copy.start()
        out_copies.append(copy)

    last = keep + STEPS - 1

    def square(r, acc):
        values = vecs[last, pl.ds(pl.multiple_of(r * 8, 8), 8), :]
        return acc + fold_lanes(values * values)

    acc = lax.fori_loop(0, rows // 8, square, jnp.zeros((8, 128), jnp.float32))
    line = lane_sum(jnp.sum(acc, axis=0, keepdims=True))
    send_row(STEPS, line, line)
    total = all_sum(STEPS, padded_count, padded_count + 8)
    norm = jnp.sqrt(total[0:1] + EPSILON)
    hess = jnp.where((lane == STEPS - 1) & (sub == last), norm, hess)
    h_out[...] = hess
    for copy in out_copies:
        copy.wait()


def group_of(count):
    for size in (4, 2):
        if count % size == 0:
            return size
    return 1


def body(basis_vectors, reaction):
    keep, planes, rows_y, width = basis_vectors.shape
    n_gx, n_gy = lax.axis_size("gx"), lax.axis_size("gy")
    g1 = group_of(n_gx)
    n1, n2 = g1 * n_gy, n_gx // g1
    size = keep + STEPS
    padded_count = -(-size // 8) * 8
    rows = planes * rows_y
    rounds = STEPS + 1
    f32 = jnp.float32
    dma = pltpu.SemaphoreType.DMA
    w, h = pl.pallas_call(
        functools.partial(kernel, keep, planes, rows_y, n_gx, n_gy, g1),
        out_shape=(
            jax.ShapeDtypeStruct((STEPS, rows, width), f32),
            jax.ShapeDtypeStruct((padded_count, 128), f32),
        ),
        in_specs=[pl.BlockSpec(memory_space=pl.ANY)] * 2,
        out_specs=(
            pl.BlockSpec(memory_space=pl.ANY),
            pl.BlockSpec(memory_space=pltpu.VMEM),
        ),
        scratch_shapes=[
            pltpu.VMEM((size, rows, width), f32),
            pltpu.VMEM((STEPS, planes + 3, rows_y + 16, width), f32),
            pltpu.VMEM((rows, width), f32),
            pltpu.VMEM((rows, width), f32),
            pltpu.VMEM((keep, padded_count, 128), f32),
            pltpu.VMEM((2, padded_count, 128), f32),
            pltpu.VMEM((rounds, n1, padded_count + 8, 128), f32),
            pltpu.VMEM((rounds, n2, padded_count + 8, 128), f32),
            pltpu.VMEM((padded_count, width), f32),
            dma((LOADS,)),
            dma((planes,)),
            dma,
            dma((STEPS,)),
            dma((STEPS, 4)),
            dma((STEPS, 4)),
            dma((rounds, n1)),
            dma((rounds, n1)),
            dma((rounds, n2)),
            dma((rounds, n2)),
        ],
        compiler_params=pltpu.CompilerParams(
            collective_id=0, has_side_effects=True, vmem_limit_bytes=48 * 1024 * 1024
        ),
    )(basis_vectors.reshape(keep, rows, width), reaction.reshape(rows, width))
    norms = jnp.stack([h[keep + j, j] for j in range(STEPS)])
    vectors = w / norms[:, None, None]
    return vectors.reshape(STEPS, planes, rows_y, width), h[:size, :STEPS]


def solution(mesh):
    in_specs = (P(None, "gx", "gy", None), P("gx", "gy", None))
    out_specs = (P(None, "gx", "gy", None), P())
    return jax.shard_map(body, mesh=mesh, in_specs=in_specs, out_specs=out_specs, check_vma=False)
```

time: 720 us -> 103 us (0.14); the launches traced: 709 us -> 103 us
  blocking collectives: 325 us -> 0 us
  matrix products: 270 us -> 0 us
  Pallas kernels: 0 us -> 96 us
  starting transfers between devices: 41.6 us -> 0 us
  other arithmetic: 33.5 us -> 3.72 us
  waiting for transfers between devices: 16.6 us -> 0 us
  local copies, waits for them, and re-layouts: 13.3 us -> 2.24 us
  between operations: 9.55 us -> 0.65 us
    psum x8 -> x0, blocking collectives: 325 us -> none  [the longest x4 167 us: body(): lax.psum(project(basis_vectors, created, image), ('gy', 'gx')) / cell_count]
    dot_general x21 -> x0, matrix products: 270 us -> none  [the longest x8 126 us: project(): jnp.einsum('kxyz,xyz->k', basis_vectors, image, precision=lax.Precision.H...]
    pallas_call x0 -> x1, Pallas kernels: none -> 96 us  [body(): pl.pallas_call(functools.partial(kernel, keep, planes, rows_y, n_gx, n_gy...]
    ppermute x16 -> x0, starting transfers between devices: 41.6 us -> none  [the longest x8 30.8 us: with_halo(): lax.ppermute(tail, axis, [(i, (i + 1) % count) for i in range(ends)])]
    ppermute x16 -> x0, waiting for transfers between devices: 16.6 us -> none  [the longest x8 9.29 us: with_halo(): lax.ppermute(head, axis, [((i + 1) % count, i) for i in range(ends)])]
    reduce_sum x7 -> x0, other arithmetic: 10.2 us -> none  [the longest x4 6.96 us: body(): jnp.sum(first_rest * first_rest)]
    another operation x16 -> x1, other arithmetic: 11.8 us -> 2.58 us  [body(): norms = jnp.stack([h[keep + j, j] for j in range(STEPS)])]
    concatenate x14 -> x0, other arithmetic: 8.46 us -> none  [the longest x6 8.17 us: project(): return jnp.concatenate([local] + extra)]
  transfers between devices with their start and end apart: 16 -> 0, of which waited for: 8 -> 0; matrix products, arithmetic and copies ran while one was open for 6% -> 0% of each run, Pallas kernels for 0% -> 0%
where the time goes in v1:
time: 103 us
  Pallas kernels  96 us (93%)
  other arithmetic  3.72 us (4%)
  local copies, waits for them, and re-layouts  2.24 us (2%)
    pallas_call x1, Pallas kernels, body(): pl.pallas_call(functools.partial(kernel, keep, planes, rows_y, n_gx, n_gy...  96 us
    another operation x1, other arithmetic, body(): norms = jnp.stack([h[keep + j, j] for j in range(STEPS)])  2.58 us

profile of v1, /device:TPU:0, one launch (start us, length us, event | category | flops | bytes accessed | tf_op | source)
XLA Modules:
  0.0 102.7 jit_solution(5457054311714519555)
XLA Ops:
  0.6 0.0 copy-start
  0.6 0.9 copy-done
  1.6 96.0 %shard_map.41 = (f32[4,256,256]{2,1,0:T(8,128)S(1)}, f32[40,128]{1,0:T(8,128)S(1)}) custom-call(f32[36,256,256]{2,1,0:T(8,128)} %bitcast.10, f32[256,256]{1,0:T(8,128)S(1)} %bitcast.8), custom_call_target="tpu_custom_call" | custom-call | tf_op jit(solution)/shard_map/pallas_call | solution.py:380
  97.6 0.7 copy.4
  98.3 0.6 fusion
  98.9 2.6 %pad_maximum_fusion = f32[4]{0:T(128)S(1)} fusion(f32[1]{0:T(128)} %bitcast.5, f32[1]{0:T(128)} %bitcast.4, f32[1]{0:T(128)} %bitcast.3, f32[1]{0:T(128)} %bitcast.2), kind=kLoop, calls=%fused_computation.1 | loop fusion | flops 12 | bytes 32 | tf_op jit(solution)/shard_map/stack | solution.py:416
  101.5 1.1 %broadcast_divide_fusion = f32[4,256,256]{2,1,0:T(8,128)} fusion(f32[4,256,256]{2,1,0:T(8,128)S(1)} %get-tuple-element.4, f32[4]{0:T(128)S(1)} %pad_maximum_fusion), kind=kLoop, calls=%fused_computation | loop fusion | flops 262144 | bytes 2097168 | tf_op jit(solution)/shard_map/div | solution.py:417
Async XLA Ops:
  0.6 1.0 copy-start

commit v2 on v1

--- a/solution.py
+++ b/solution.py
@@ -135,16 +135,21 @@
             for n, (src, dst) in enumerate(refs)
         ]
 
-    def start_halo(step):
-        for n, copy in enumerate(halo_copies(step)):
+    def start_halo(step, which):
+        copies = halo_copies(step)
+        for n in which:
+            copy = copies[n]
+
             @pl.when(sides[n][0])
             def _(copy=copy):
                 copy.start()
 
-    def wait_halo(step):
+    def wait_halo(step, which):
         copies = halo_copies(step)
         arrives = (has_xl, has_xh, has_yl, has_yh)
-        for n, copy in enumerate(copies):
+        for n in which:
+            copy = copies[n]
+
             @pl.when(arrives[n])
             def _(copy=copy):
                 copy.wait_recv()
@@ -153,7 +158,12 @@
             def _(copy=copy):
                 copy.wait_send()
 
-    def exchange(rnd, slots, me, count, member, send, recv, start, stop):
+    stage1 = (slots1, me1, n1, member1, send1, recv1)
+    stage2 = (slots2, me2, n2, member2, send2, recv2)
+
+    def exchange(rnd, stage, start, stop, begin):
+        slots, me, count, member, send, recv = stage
+
         def copy_of(slot, d):
             return pltpu.make_async_remote_copy(
                 src_ref=slots.at[rnd, slot, start:stop], dst_ref=slots.at[rnd, slot, start:stop],
@@ -161,8 +171,10 @@
                 device_id=member(d)[1], device_id_type=MESH,
             )
 
-        for d in range(1, count):
-            copy_of(me, d).start()
+        if begin:
+            for d in range(1, count):
+                copy_of(me, d).start()
+            return None
         for d in range(1, count):
             copy_of(member(d)[0], d).wait_recv()
         for d in range(1, count):
@@ -172,12 +184,20 @@
             total = total + slots[rnd, slot, start:stop]
         return total
 
+    def begin1(rnd, start, stop):
+        exchange(rnd, stage1, start, stop, True)
+
+    def begin2(rnd, start, stop):
+        slots2[rnd, me2, start:stop] = exchange(rnd, stage1, start, stop, False)
+        exchange(rnd, stage2, start, stop, True)
+
+    def finish(rnd, start, stop):
+        return exchange(rnd, stage2, start, stop, False) / cells
+
     def all_sum(rnd, start, stop):
-        total = exchange(rnd, slots1, me1, n1, member1, send1, recv1, start, stop)
-        if n2 > 1:
-            slots2[rnd, me2, start:stop] = total
-            total = exchange(rnd, slots2, me2, n2, member2, send2, recv2, start, stop)
-        return total / cells
+        begin1(rnd, start, stop)
+        begin2(rnd, start, stop)
+        return finish(rnd, start, stop)
 
     shape = (padded_count, 128)
     lane = lax.broadcasted_iota(jnp.int32, shape, 1)
@@ -234,18 +254,24 @@
             total = total - (0.5 * sz) * jnp.where(lanes >= 2, roll(here, 2, 1), 0.0)
             image[out_at, :] = total
 
-        @pl.loop(0, planes)
-        def _(p):
+        inner = range(2, planes - 1)
+        wait_halo(step, (2, 3))
+        for p in inner:
             @pl.loop(0, rows_y // tall)
-            def _(q):
+            def _(q, p=p):
                 piece(p, q)
 
+        wait_halo(step, (0, 1))
+        for p in [p for p in range(planes) if p not in inner]:
+            @pl.loop(0, rows_y // tall)
+            def _(q, p=p):
+                piece(p, q)
+
     def combine(step, count, scale):
-        tall = 16
+        tall = 32 if rows_y % 32 == 0 else 16
         scale_row = jnp.concatenate([scale] * (width // 128), axis=1)
 
-        @pl.loop(0, planes)
-        def _(p):
+        def plane(p):
             @pl.loop(0, rows_y // tall)
             def _(q):
                 at = pl.ds(pl.multiple_of(p * rows_y + q * tall, 8), tall)
@@ -256,6 +282,16 @@
                 if step < STEPS - 1:
                     padded[step + 1, p + 2, pl.ds(pl.multiple_of(q * tall + 8, 8), tall), :] = total
 
+        more = step < STEPS - 1
+        done = []
+        for part, side in (((planes - 2, planes - 1), 0), ((0,), 1), (range(planes), 2)):
+            for p in part:
+                if p not in done:
+                    plane(p)
+                    done.append(p)
+            if more:
+                start_halo(step + 1, (side,) if side < 2 else (2, 3))
+
     def send_row(rnd, a_row, b_row):
         slots1[rnd, me1, padded_count : padded_count + 8] = jnp.where(
             sub8 == 0, a_row, jnp.where(sub8 == 1, b_row, 0.0)
@@ -263,7 +299,7 @@
 
     for copy in last_copies:
         copy.wait()
-    start_halo(0)
+    start_halo(0, (0, 1, 2, 3))
     ready = 0
     blocks = [(s, min(s + BLOCK, keep)) for s in range(0, keep, BLOCK)]
     for jb in range(len(blocks)):
@@ -296,8 +332,9 @@
     local_gram = jnp.zeros(shape, jnp.float32)
     for i in range(keep):
         local_gram = jnp.where(lane == i, lane_sum(gram_rows[i]), local_gram)
-    slots1[0, me1, 0:padded_count] = local_gram
+    slots1[STEPS + 1, me1, 0:padded_count] = local_gram
     react_copy.wait()
+    begin1(STEPS + 1, 0, padded_count)
 
     gram = None
     scales = jnp.ones(shape, jnp.float32)
@@ -310,14 +347,15 @@
         if step > 0:
             project(lambda at: vecs[last, at, :], count, 1)
             b_row = to_row(lane_sum(proj_rows[1]))
-        wait_halo(step)
         stencil(step)
         project(lambda at: image[at, :], count, 0)
         send_row(step, to_row(lane_sum(proj_rows[0])), b_row)
         if step == 0:
-            total = all_sum(0, 0, padded_count + 8)
-            gram = total[0:padded_count]
-            total = total[padded_count:]
+            begin1(0, padded_count, padded_count + 8)
+            begin2(STEPS + 1, 0, padded_count)
+            begin2(0, padded_count, padded_count + 8)
+            gram = finish(STEPS + 1, 0, padded_count)
+            total = finish(0, padded_count, padded_count + 8)
             scale = jnp.ones((1, 128), jnp.float32)
         else:
             total = all_sum(step, padded_count, padded_count + 8)
@@ -336,8 +374,6 @@
         scaled = weights * scales
         coef[...] = jnp.concatenate([scaled] * (width // 128), axis=1)
         combine(step, count, scale)
-        if step < STEPS - 1:
-            start_halo(step + 1)
         copy = pltpu.make_async_copy(vecs.at[keep + step], w_out.at[step], out_sem.at[step])
         copy.start()
         out_copies.append(copy)
@@ -374,7 +410,7 @@
     size = keep + STEPS
     padded_count = -(-size // 8) * 8
     rows = planes * rows_y
-    rounds = STEPS + 1
+    rounds = STEPS + 2
     f32 = jnp.float32
     dma = pltpu.SemaphoreType.DMA
     w, h = pl.pallas_call(

time: 103 us -> 98.5 us (0.956)
  Pallas kernels: 96 us -> 91.7 us
    pallas_call x1, Pallas kernels: 96 us -> 91.7 us  [body(): pl.pallas_call(functools.partial(kernel, keep, planes, rows_y, n_gx, n_gy...]
where the time goes in v2:
time: 98.5 us; the launch traced here: 98.3 us
  Pallas kernels  91.7 us (93%)
  other arithmetic  3.72 us (4%)
  local copies, waits for them, and re-layouts  2.24 us (2%)
    pallas_call x1, Pallas kernels, body(): pl.pallas_call(functools.partial(kernel, keep, planes, rows_y, n_gx, n_gy...  91.7 us
    another operation x1, other arithmetic, body(): norms = jnp.stack([h[keep + j, j] for j in range(STEPS)])  2.58 us

profile of v2, /device:TPU:0, one launch (start us, length us, event | category | flops | bytes accessed | tf_op | source)
XLA Modules:
  0.0 98.3 jit_solution(16986386852720358098)
XLA Ops:
  0.6 0.0 copy-start
  0.6 0.9 copy-done
  1.6 91.7 %shard_map.41 = (f32[4,256,256]{2,1,0:T(8,128)S(1)}, f32[40,128]{1,0:T(8,128)S(1)}) custom-call(f32[36,256,256]{2,1,0:T(8,128)} %bitcast.10, f32[256,256]{1,0:T(8,128)S(1)} %bitcast.8), custom_call_target="tpu_custom_call" | custom-call | tf_op jit(solution)/shard_map/pallas_call | solution.py:416
  93.3 0.7 copy.4
  93.9 0.6 fusion
  94.6 2.6 %pad_maximum_fusion = f32[4]{0:T(128)S(1)} fusion(f32[1]{0:T(128)} %bitcast.5, f32[1]{0:T(128)} %bitcast.4, f32[1]{0:T(128)} %bitcast.3, f32[1]{0:T(128)} %bitcast.2), kind=kLoop, calls=%fused_computation.1 | loop fusion | flops 12 | bytes 32 | tf_op jit(solution)/shard_map/stack | solution.py:452
  97.1 1.1 %broadcast_divide_fusion = f32[4,256,256]{2,1,0:T(8,128)} fusion(f32[4,256,256]{2,1,0:T(8,128)S(1)} %get-tuple-element.4, f32[4]{0:T(128)S(1)} %pad_maximum_fusion), kind=kLoop, calls=%fused_computation | loop fusion | flops 262144 | bytes 2097168 | tf_op jit(solution)/shard_map/div | solution.py:453
Async XLA Ops:
  0.6 1.0 copy-start

commit v3 on v2

--- a/solution.py
+++ b/solution.py
@@ -226,7 +226,7 @@
                 )
 
             zero = jnp.zeros((8, 128), jnp.float32)
-            sums = lax.fori_loop(0, rows // 8, step, (zero,) * len(group))
+            sums = lax.fori_loop(0, rows // 8, step, (zero,) * len(group), unroll=4)
             for i, acc in zip(group, sums):
                 proj_rows[kind, i : i + 1, :] = jnp.sum(acc, axis=0, keepdims=True)
 
@@ -257,13 +257,13 @@
         inner = range(2, planes - 1)
         wait_halo(step, (2, 3))
         for p in inner:
-            @pl.loop(0, rows_y // tall)
+            @pl.loop(0, rows_y // tall, unroll=True)
             def _(q, p=p):
                 piece(p, q)
 
         wait_halo(step, (0, 1))
         for p in [p for p in range(planes) if p not in inner]:
-            @pl.loop(0, rows_y // tall)
+            @pl.loop(0, rows_y // tall, unroll=True)
             def _(q, p=p):
                 piece(p, q)
 

time: 98.5 us -> 93.4 us (0.948)
  Pallas kernels: 91.7 us -> 86.6 us
    pallas_call x1, Pallas kernels: 91.7 us -> 86.6 us  [body(): pl.pallas_call(functools.partial(kernel, keep, planes, rows_y, n_gx, n_gy...]
where the time goes in v3:
time: 93.4 us; the launch traced here: 93.2 us
  Pallas kernels  86.6 us (93%)
  other arithmetic  3.72 us (4%)
  local copies, waits for them, and re-layouts  2.24 us (2%)
    pallas_call x1, Pallas kernels, body(): pl.pallas_call(functools.partial(kernel, keep, planes, rows_y, n_gx, n_gy...  86.6 us
    another operation x1, other arithmetic, body(): norms = jnp.stack([h[keep + j, j] for j in range(STEPS)])  2.58 us

profile of v3, /device:TPU:0, one launch (start us, length us, event | category | flops | bytes accessed | tf_op | source)
XLA Modules:
  0.0 93.2 jit_solution(2845265465172320896)
XLA Ops:
  0.6 0.0 copy-start
  0.6 0.9 %copy-done = f32[4,64,256]{2,1,0:T(8,128)S(1)} copy-done((f32[4,64,256]{2,1,0:T(8,128)S(1)}, f32[4,64,256]{2,1,0:T(8,128)}, u32[]{:S(2)}) %copy-start) | copy-done | bytes 262168
  1.6 86.6 %shard_map.41 = (f32[4,256,256]{2,1,0:T(8,128)S(1)}, f32[40,128]{1,0:T(8,128)S(1)}) custom-call(f32[36,256,256]{2,1,0:T(8,128)} %bitcast.10, f32[256,256]{1,0:T(8,128)S(1)} %bitcast.8), custom_call_target="tpu_custom_call" | custom-call | tf_op jit(solution)/shard_map/pallas_call | solution.py:416
  88.2 0.7 copy.4
  88.9 0.6 fusion
  89.5 2.6 %pad_maximum_fusion = f32[4]{0:T(128)S(1)} fusion(f32[1]{0:T(128)} %bitcast.5, f32[1]{0:T(128)} %bitcast.4, f32[1]{0:T(128)} %bitcast.3, f32[1]{0:T(128)} %bitcast.2), kind=kLoop, calls=%fused_computation.1 | loop fusion | flops 12 | bytes 32 | tf_op jit(solution)/shard_map/stack | solution.py:452
  92.1 1.1 %broadcast_divide_fusion = f32[4,256,256]{2,1,0:T(8,128)} fusion(f32[4,256,256]{2,1,0:T(8,128)S(1)} %get-tuple-element.4, f32[4]{0:T(128)S(1)} %pad_maximum_fusion), kind=kLoop, calls=%fused_computation | loop fusion | flops 262144 | bytes 2097168 | tf_op jit(solution)/shard_map/div | solution.py:453
Async XLA Ops:
  0.6 1.0 %copy-start = (f32[4,64,256]{2,1,0:T(8,128)S(1)}, f32[4,64,256]{2,1,0:T(8,128)}, u32[]{:S(2)}) copy-start(f32[4,64,256]{2,1,0:T(8,128)} %param.3) | copy-start | bytes 786436
